TPU v7x, 32 devices: a whole 2x2x4 slice. The times are simulated.
32 devices in a mesh: section: 2 (over core), dp: 4 (over y, x), tensor: 4 (over z).
Axes of the slice: x: 2, y: 2, z: 4, core: 2. Of those that a mesh axis runs over, the one named last changes fastest.
Arguments:
- tokens_in: bfloat16 [512, 8192], P('dp', ('section', 'tensor')), may hold values from -70 to 70
- gain_attn: bfloat16 [8192], replicated, may hold values from 0.5 to 1.5
- w_query: bfloat16 [8192, 8192], P(None, ('section', 'tensor')), may hold values from -6 to 6
- w_keyval: bfloat16 [8192, 2048], P(None, ('section', 'tensor')), may hold values from -0.0625 to 0.0625
- w_out: bfloat16 [8192, 8192], P(('section', 'tensor')), may hold values from -0.0625 to 0.0625
- gain_mlp: bfloat16 [8192], replicated, may hold values from 0.5 to 1.5
- w_gate: bfloat16 [8192, 16384], P('dp', ('section', 'tensor')), may hold values from -0.0625 to 0.0625
- w_up: bfloat16 [8192, 16384], P('dp', ('section', 'tensor')), may hold values from -0.0625 to 0.0625
- w_down: bfloat16 [16384, 8192], P(('section', 'tensor'), 'dp'), may hold values from -0.046875 to 0.046875
Outputs:
- layer_out: bfloat16 [512, 8192], P(('section', 'tensor'), 'dp')
All inputs are finite; a program needn't handle non-finite values.
Results may differ from a plain program's by a relative error of at most 0.0068.
Values may be sent and summed in bfloat16 or wider, within the bound.
A program may use at most 128 MiB of HBM per device.

v0:
```python
import jax
import jax.numpy as jnp
from jax import lax
from jax.sharding import PartitionSpec as P

H = 64
KVH = 8
HD = 128
EPS = 1e-05
THETA = 10000.0


def rms_scale(row_data, gain_row):
    values = row_data.astype(jnp.float32)
    factor = lax.rsqrt(jnp.mean(values * values, axis=-1, keepdims=True) + EPS)
    return (values * factor * gain_row.astype(jnp.float32)).astype(jnp.bfloat16)


def rotary(values, positions):
    half_dim = values.shape[-1] // 2
    frequency = THETA ** (-jnp.arange(half_dim, dtype=jnp.float32) * 2.0 / values.shape[-1])
    angles = positions.astype(jnp.float32)[:, None] * frequency[None, :]
    cosine = jnp.cos(angles)[:, None, :]
    sine_part = jnp.sin(angles)[:, None, :]
    first_half = values[..., :half_dim]
    second = values[..., half_dim:]
    return jnp.concatenate(
        [first_half * cosine - second * sine_part, second * cosine + first_half * sine_part],
        axis=-1,
    )


def shards(tokens_in, gain_attn, w_query, w_keyval, w_out, gain_mlp, w_gate, w_up, w_down):
    group_count = lax.axis_size(("section", "tensor"))
    group_index = lax.axis_index(("section", "tensor"))
    data_index = lax.axis_index("dp")
    local_rows = tokens_in.shape[0]
    full_rows = lax.all_gather(tokens_in, ("section", "tensor"), axis=1, tiled=True)
    normed_attn = rms_scale(full_rows, gain_attn)
    heads_dev = w_query.shape[1] // HD
    group_size = H // KVH
    kv_dev = max(1, heads_dev // group_size)
    positions_local = data_index * local_rows + jnp.arange(local_rows, dtype=jnp.int32)
    query_proj = jnp.dot(normed_attn, w_query, preferred_element_type=jnp.float32)
    query_rot = rotary(query_proj.reshape(local_rows, heads_dev, HD), positions_local).astype(
        jnp.bfloat16
    )
    keyval_part = jnp.dot(normed_attn, w_keyval, preferred_element_type=jnp.float32).astype(
        jnp.bfloat16
    )
    keyval_rows = lax.all_gather(keyval_part, ("section", "tensor"), axis=1, tiled=True)
    first_kv = group_index * heads_dev // group_size
    key_cols = lax.dynamic_slice_in_dim(keyval_rows, first_kv * HD, kv_dev * HD, 1)
    value_cols = lax.dynamic_slice_in_dim(keyval_rows, KVH * HD + first_kv * HD, kv_dev * HD, 1)
    needed = jnp.concatenate([key_cols, value_cols], axis=1)
    kv_all = lax.all_gather(needed, "dp", axis=0, tiled=True)
    total_rows = kv_all.shape[0]
    key_pos = jnp.arange(total_rows, dtype=jnp.int32)
    key_rot = rotary(
        kv_all[:, : kv_dev * HD].astype(jnp.float32).reshape(total_rows, kv_dev, HD), key_pos
    ).astype(jnp.bfloat16)
    value_all = kv_all[:, kv_dev * HD :].reshape(total_rows, kv_dev, HD)
    query_grp = query_rot.reshape(local_rows, kv_dev, heads_dev // kv_dev, HD)
    scores = jnp.einsum(
        "rkgd,skd->kgrs", query_grp, key_rot, preferred_element_type=jnp.float32
    ) * HD ** (-0.5)
    allowed = key_pos[None, :] <= positions_local[:, None]
    scores = jnp.where(allowed[None, None, :, :], scores, -1e30)
    row_peak = jnp.max(scores, axis=-1, keepdims=True)
    expo_rows = jnp.exp(scores - row_peak)
    prob_rows = (expo_rows / jnp.sum(expo_rows, axis=-1, keepdims=True)).astype(jnp.bfloat16)
    attended = jnp.einsum(
        "kgrs,skd->rkgd", prob_rows, value_all, preferred_element_type=jnp.float32
    )
    attended = attended.astype(jnp.bfloat16).reshape(local_rows, heads_dev * HD)
    head_terms = jnp.dot(attended, w_out, preferred_element_type=jnp.float32)
    summed = lax.psum(head_terms, ("section", "tensor"))
    mid_full = (full_rows.astype(jnp.float32) + summed).astype(jnp.bfloat16)
    normed_mlp = rms_scale(mid_full, gain_mlp)
    mid_cols, norm_cols = (
        lax.all_to_all(mid_full, "dp", split_axis=1, concat_axis=0, tiled=True),
        lax.all_to_all(normed_mlp, "dp", split_axis=1, concat_axis=0, tiled=True),
    )
    hidden_width = w_gate.shape[1]
    row_block = norm_cols
    gate_block = jnp.dot(row_block, w_gate, preferred_element_type=jnp.float32)
    up_block = jnp.dot(row_block, w_up, preferred_element_type=jnp.float32)
    gate_both = lax.psum_scatter(
        jnp.concatenate([gate_block, up_block], axis=1), "dp", scatter_dimension=0, tiled=True
    )
    hidden_part = (jax.nn.silu(gate_both[:, :hidden_width]) * gate_both[:, hidden_width:]).astype(
        jnp.bfloat16
    )
    hidden_all = lax.all_gather(hidden_part, "dp", axis=0, tiled=True)
    out_rows = hidden_all.shape[0] // group_count
    row_block = hidden_all
    down_part = lax.psum_scatter(
        jnp.dot(row_block, w_down, preferred_element_type=jnp.float32),
        ("section", "tensor"),
        scatter_dimension=0,
        tiled=True,
    )
    resid_rows = lax.dynamic_slice_in_dim(mid_cols, group_index * out_rows, out_rows, 0)
    return (resid_rows.astype(jnp.float32) + down_part).astype(jnp.bfloat16)


def solution(mesh):
    placed = (
        P("dp", ("section", "tensor")),
        P(),
        P(None, ("section", "tensor")),
        P(None, ("section", "tensor")),
        P(("section", "tensor"), None),
        P(),
        P("dp", ("section", "tensor")),
        P("dp", ("section", "tensor")),
        P(("section", "tensor"), "dp"),
    )
    return jax.shard_map(
        shards,
        mesh=mesh,
        in_specs=placed,
        out_specs=P(("section", "tensor"), "dp"),
        check_vma=False,
    )
```

profile of v0, /device:TPU:0, one launch (start us, length us, event | category | flops | bytes accessed | tf_op | source)
XLA Modules:
  0.0 471.4 jit_solution(17559355887173237044)
XLA Ops:
  8.5 32.4 %all-gather.3.cloned.1.call-done = bf16[128,8192]{1,0:T(8,128)(2,1)} async-done(((bf16[128,1024]{1,0:T(8,128)(2,1)}), bf16[128,8192]{1,0:T(8,128)(2,1)}) %all-gather.3.cloned.1.call-update) | async-done | bytes 2097168 | tf_op jit(solution)/shard_map/all_gather | solution.py:38
  40.8 2.1 fusion.3
  42.9 3.7 convolution_convert_fusion.1
  46.7 26.2 %all_gather.13 = bf16[128,2048]{1,0:T(8,128)(2,1)S(1)} all-gather(bf16[128,256]{1,0:T(8,128)(2,1)S(1)} %convolution_convert_fusion.1), channel_id=1, replica_groups=mesh['section'=2,'dp'=4,'tensor'=4] {'section','tensor'}, dimensions={1}, use_global_device_ids=true | all-gather | bytes 589824 | tf_op jit(solution)/shard_map/all_gather | solution.py:51
  72.9 9.0 %all_gather.14 = bf16[512,256]{1,0:T(8,128)(2,1)S(1)} all-gather(bf16[128,256]{1,0:T(8,128)(2,1)S(1)} %pad_maximum_fusion.1), channel_id=1, replica_groups=mesh['section'=2,'dp'=4,'tensor'=4] {'dp'}, dimensions={0}, use_global_device_ids=true | all-gather | bytes 327680 | tf_op jit(solution)/shard_map/all_gather | solution.py:56
  81.9 8.4 %convolution_bitcast_fusion = f32[16,8,8,128]{3,1,2,0:T(8,128)S(1)} fusion(bf16[8192,1024]{1,0:T(8,128)(2,1)} %param.11, bf16[128,8192]{1,0:T(8,128)(2,1)S(1)} %copy-done, f32[8192]{0:T(1024)S(1)} %convert_element_type.75, f32[128]{0:T(128)S(1)} %add_rsqrt_fusion.1), kind=kOutput, calls=%fused_computation.19 | convolution fusion | flops 2151677952 | bytes 19431936 | tf_op jit(solution)/shard_map/dot_general | solution.py:44
  90.7 1.2 fusion.27
  93.6 0.7 slice-done.3
  94.3 4.8 %fusion.33 = f32[128,8192]{1,0:T(8,128)} fusion(bf16[128,1024]{0,1:T(8,128)(2,1)S(1)} %bitcast.66, bf16[1024,8192]{1,0:T(8,128)(2,1)S(1)} %bitcast.58), kind=kOutput, calls=%fused_computation.64 | convolution fusion | flops 2147483648 | bytes 21233664 | tf_op jit(solution)/shard_map/dot_general | solution.py:76
  99.9 94.9 %all-reduce.2.cloned.1.call-done = f32[128,8192]{1,0:T(8,128)} async-done(((f32[128,8192]{1,0:T(8,128)}), f32[128,8192]{1,0:T(8,128)}) %all-reduce.2.cloned.1.call-update) | async-done | bytes 4194320 | tf_op jit(solution)/shard_map/psum | solution.py:77
  194.8 3.7 fusion
  199.4 28.8 %all_to_all.38 = bf16[128,4,2048]{2,0,1:T(8,128)(2,1)S(1)} all-to-all(bf16[128,4,2048]{2,0,1:T(8,128)(2,1)S(1)} %bitcast.61), channel_id=1, replica_groups=mesh['section'=2,'dp'=4,'tensor'=4] {'dp'}, dimensions={1} | all-to-all | bytes 4194304 | tf_op jit(solution)/shard_map/all_to_all | solution.py:82
  228.3 4.6 fusion.35
  232.9 4.6 fusion.34
  237.5 3.8 pad_maximum_fusion
  241.4 85.1 %reduce-scatter.3.cloned.1.call-done = f32[128,4096]{1,0:T(8,128)} async-done(((f32[512,4096]{1,0:T(8,128)}), f32[128,4096]{1,0:T(8,128)}) %reduce-scatter.3.cloned.1.call-update) | async-done | bytes 2097168 | tf_op jit(solution)/shard_map/reduce_scatter | solution.py:88
  326.5 2.6 fusion.8
  329.2 35.3 %all-gather.5.cloned.1.call-done = bf16[512,2048]{1,0:T(8,128)(2,1)} async-done(((bf16[128,2048]{1,0:T(8,128)(2,1)}), bf16[512,2048]{1,0:T(8,128)(2,1)}) %all-gather.5.cloned.1.call-update) | async-done | bytes 2097168 | tf_op jit(solution)/shard_map/all_gather | solution.py:94
  364.5 10.5 %fusion.36 = f32[512,2048]{1,0:T(8,128)} fusion(bf16[512,2048]{1,0:T(8,128)(2,1)} %all-gather.5.cloned.1.call-done, bf16[2048,2048]{1,0:T(8,128)(2,1)} %param.17), kind=kOutput, calls=%fused_computation.67 | convolution fusion | flops 4294967296 | bytes 14680064 | tf_op jit(solution)/shard_map/dot_general | solution.py:98
  374.9 1.5 copy.42
  376.4 3.6 all-to-all-start
  380.0 24.9 %all-to-all-done = bf16[128,4,2048]{2,0,1:T(8,128)(2,1)S(1)} async-done(((bf16[128,4,2048]{2,0,1:T(8,128)(2,1)}), bf16[128,4,2048]{2,0,1:T(8,128)(2,1)S(1)}, u32[]{:S(2)}, u32[]{:S(2)}) %all-to-all-start) | async-done | bytes 2097184 | tf_op jit(solution)/shard_map/all_to_all | solution.py:81
  405.0 58.1 %reduce-scatter.5.cloned.1.call-done = f32[64,2048]{1,0:T(8,128)} async-done(((f32[512,2048]{1,0:T(8,128)}), f32[64,2048]{1,0:T(8,128)}) %reduce-scatter.5.cloned.1.call-update) | async-done | bytes 524304 | tf_op jit(solution)/shard_map/reduce_scatter | solution.py:97
  463.1 1.8 add_convert_fusion
  (53 shorter events, 5.6 us)
Async XLA Ops:
  6.5 34.3 %all-gather.3.cloned.1.call-start = ((), (), s32[]{:S(2)}) async-start(), calls=%async_computation.4 | async-start | bytes 2359296 | tf_op jit(solution)/shard_map/all_gather | solution.py:38
  7.3 187.5 %all-reduce.2.cloned.1.call-start = ((), (), s32[]{:S(2)}) async-start(), calls=%async_computation.5 | async-start | bytes 8388608 | tf_op jit(solution)/shard_map/psum | solution.py:77
  42.9 39.0 %copy-start = (bf16[128,8192]{1,0:T(8,128)(2,1)S(1)}, bf16[128,8192]{1,0:T(8,128)(2,1)}, u32[]{:S(2)}) copy-start(bf16[128,8192]{1,0:T(8,128)(2,1)} %all-gather.3.cloned.1.call-done) | copy-start | bytes 6291460
  81.9 11.6 %slice-start = ((s8[16777216]{0:T(1024)(128)(4,1)}), s8[4194304]{0:T(1024)(128)(4,1)S(1)}, s32[]{:S(2)}) async-start(s8[16777216]{0:T(1024)(128)(4,1)} %bitcast.57), calls=%async_computation.9 | async-start | bytes 8388608
  81.9 11.6 %slice-start.1 = ((s8[16777216]{0:T(1024)(128)(4,1)}), s8[4194304]{0:T(1024)(128)(4,1)S(1)}, s32[]{:S(2)}) async-start(s8[16777216]{0:T(1024)(128)(4,1)} %bitcast.57), calls=%async_computation.10 | async-start | bytes 8388608
  81.9 11.6 %slice-start.2 = ((s8[16777216]{0:T(1024)(128)(4,1)}), s8[4194304]{0:T(1024)(128)(4,1)S(1)}, s32[]{:S(2)}) async-start(s8[16777216]{0:T(1024)(128)(4,1)} %bitcast.57), calls=%async_computation.11 | async-start | bytes 8388608
  92.1 2.2 slice-start.3
  99.1 0.7 copy-start.1
  99.2 227.3 %reduce-scatter.3.cloned.1.call-start = ((), (), s32[]{:S(2)}) async-start(), calls=%async_computation.6 | async-start | bytes 10485760 | tf_op jit(solution)/shard_map/reduce_scatter | solution.py:88
  194.8 33.5 %slice-start.4 = ((s8[8388608]{0:T(1024)(128)(4,1)}), s8[4194304]{0:T(1024)(128)(4,1)S(1)}, s32[]{:S(2)}) async-start(s8[8388608]{0:T(1024)(128)(4,1)} %bitcast.67), calls=%async_computation.13 | async-start | bytes 8388608
  198.5 29.8 %slice-start.5 = ((s8[8388608]{0:T(1024)(128)(4,1)}), s8[4194304]{0:T(1024)(128)(4,1)S(1)}, s32[]{:S(2)}) async-start(s8[8388608]{0:T(1024)(128)(4,1)} %bitcast.67), calls=%async_computation.14 | async-start | bytes 8388608
  199.4 33.5 %slice-start.6 = ((s8[8388608]{0:T(1024)(128)(4,1)}), s8[4194304]{0:T(1024)(128)(4,1)S(1)}, s32[]{:S(2)}) async-start(s8[8388608]{0:T(1024)(128)(4,1)} %bitcast.69), calls=%async_computation.15 | async-start | bytes 8388608
  228.3 4.6 slice-start.7
  241.3 123.2 %all-gather.5.cloned.1.call-start = ((), (), s32[]{:S(2)}) async-start(), calls=%async_computation.7 | async-start | bytes 2621440 | tf_op jit(solution)/shard_map/all_gather | solution.py:94
  329.1 133.9 %reduce-scatter.5.cloned.1.call-start = ((), (), s32[]{:S(2)}) async-start(), calls=%async_computation.8 | async-start | bytes 4718592 | tf_op jit(solution)/shard_map/reduce_scatter | solution.py:97
  376.4 28.6 %all-to-all-start = ((bf16[128,4,2048]{2,0,1:T(8,128)(2,1)}), bf16[128,4,2048]{2,0,1:T(8,128)(2,1)S(1)}, u32[]{:S(2)}, u32[]{:S(2)}) async-start(bf16[128,4,2048]{2,0,1:T(8,128)(2,1)} %bitcast.59), calls=%async_computation | async-start | bytes 4194304 | tf_op jit(solution)/shard_map/all_to_all | solution.py:81
Sparse Core Ops, SparseCore 0:
  8.9 31.8 all-gather.2
  99.3 95.4 all-reduce.1
  241.4 85.0 reduce-scatter.2
  329.3 35.1 all-gather.4
  375.1 87.9 reduce-scatter.4
where the time goes:
time: 472 us; the launch traced here: 471 us
  waiting for transfers between devices  332 us (70%)
  blocking collectives  64 us (14%)
  matrix products  37.7 us (8%)
  other arithmetic  17.5 us (4%)
  between operations  13.5 us (3%)
    psum x1, waiting for transfers between devices, shards(): summed = lax.psum(head_terms, ('section', 'tensor'))  94.9 us
    reduce_scatter x1, waiting for transfers between devices, shards(): lax.psum_scatter(jnp.concatenate([gate_block, up_block], axis=1), 'dp', s...  85.1 us
    reduce_scatter x1, waiting for transfers between devices, shards(): lax.psum_scatter(jnp.dot(row_block, w_down, preferred_element_type=jnp.fl...  58.1 us
    all_gather x1, waiting for transfers between devices, shards(): hidden_all = lax.all_gather(hidden_part, 'dp', axis=0, tiled=True)  35.3 us
    all_gather x1, waiting for transfers between devices, shards(): lax.all_gather(tokens_in, ('section', 'tensor'), axis=1, tiled=True)  32.4 us
    all_to_all x1, blocking collectives, shards(): lax.all_to_all(normed_mlp, 'dp', split_axis=1, concat_axis=0, tiled=True)  28.8 us
    all_gather x1, blocking collectives, shards(): lax.all_gather(keyval_part, ('section', 'tensor'), axis=1, tiled=True)  26.2 us
    all_to_all x1, waiting for transfers between devices, shards(): lax.all_to_all(mid_full, 'dp', split_axis=1, concat_axis=0, tiled=True)  24.9 us
  transfers between devices with their start and end apart: 6, of which 6 were waited for; matrix products, arithmetic and copies ran while one was open for 1% of the time, Pallas kernels for 0%

commit v1 on v0

--- a/solution.py
+++ b/solution.py
@@ -74,7 +74,7 @@
     )
     attended = attended.astype(jnp.bfloat16).reshape(local_rows, heads_dev * HD)
     head_terms = jnp.dot(attended, w_out, preferred_element_type=jnp.float32)
-    summed = lax.psum(head_terms, ("section", "tensor"))
+    summed = jnp.sum(lax.all_gather(head_terms, ("section", "tensor")), axis=0)
     mid_full = (full_rows.astype(jnp.float32) + summed).astype(jnp.bfloat16)
     normed_mlp = rms_scale(mid_full, gain_mlp)
     mid_cols, norm_cols = (

time: 472 us -> 693 us (1.47)
  waiting for transfers between devices: 332 us -> 522 us
  other arithmetic: 17.5 us -> 32.7 us
  local copies, waits for them, and re-layouts: 3.48 us -> 11.2 us
    all_gather x0 -> x1, waiting for transfers between devices: none -> 287 us  [shards(): summed = jnp.sum(lax.all_gather(head_terms, ('section', 'tensor')), axis=0)]
    psum x1 -> x0, waiting for transfers between devices: 94.9 us -> none  [shards(): summed = lax.psum(head_terms, ('section', 'tensor'))]
    reduce_sum x0 -> x1, other arithmetic: none -> 14 us  [shards(): summed = jnp.sum(lax.all_gather(head_terms, ('section', 'tensor')), axis=0)]
  transfers between devices with their start and end apart: 6 -> 6, of which waited for: 6 -> 6; matrix products, arithmetic and copies ran while one was open for 1% -> 0% of each run, Pallas kernels for 0% -> 0%
where the time goes in v1:
time: 693 us; the launch traced here: 692 us
  waiting for transfers between devices  522 us (75%)
  blocking collectives  65.7 us (9%)
  matrix products  44 us (6%)
  other arithmetic  32.7 us (5%)
  between operations  13.4 us (2%)
  local copies, waits for them, and re-layouts  11.2 us (2%)
    all_gather x1, waiting for transfers between devices, shards(): summed = jnp.sum(lax.all_gather(head_terms, ('section', 'tensor')), axis=0)  287 us
    reduce_scatter x1, waiting for transfers between devices, shards(): lax.psum_scatter(jnp.concatenate([gate_block, up_block], axis=1), 'dp', s...  83.1 us
    reduce_scatter x1, waiting for transfers between devices, shards(): lax.psum_scatter(jnp.dot(row_block, w_down, preferred_element_type=jnp.fl...  58.1 us
    all_gather x1, waiting for transfers between devices, shards(): hidden_all = lax.all_gather(hidden_part, 'dp', axis=0, tiled=True)  35.3 us
    all_gather x1, waiting for transfers between devices, shards(): lax.all_gather(tokens_in, ('section', 'tensor'), axis=1, tiled=True)  32.4 us
    all_to_all x1, blocking collectives, shards(): lax.all_to_all(normed_mlp, 'dp', split_axis=1, concat_axis=0, tiled=True)  30.5 us
    all_gather x1, blocking collectives, shards(): lax.all_gather(keyval_part, ('section', 'tensor'), axis=1, tiled=True)  26.2 us
    all_to_all x1, waiting for transfers between devices, shards(): lax.all_to_all(mid_full, 'dp', split_axis=1, concat_axis=0, tiled=True)  24.9 us
  transfers between devices with their start and end apart: 6, of which 6 were waited for; matrix products, arithmetic and copies ran while one was open for 0% of the time, Pallas kernels for 0%

profile of v1, /device:TPU:0, one launch (start us, length us, event | category | flops | bytes accessed | tf_op | source)
XLA Modules:
  0.0 692.4 jit_solution(8643388113371828054)
XLA Ops:
  8.5 32.4 %all-gather.5.cloned.1.call-done = bf16[128,8192]{1,0:T(8,128)(2,1)} async-done(((bf16[128,1024]{1,0:T(8,128)(2,1)}), bf16[128,8192]{1,0:T(8,128)(2,1)}) %all-gather.5.cloned.1.call-update) | async-done | bytes 2097168 | tf_op jit(solution)/shard_map/all_gather | solution.py:38
  40.8 2.1 fusion.3
  42.9 3.7 convolution_convert_fusion.1
  46.7 26.2 %all_gather.19 = bf16[128,2048]{1,0:T(8,128)(2,1)S(1)} all-gather(bf16[128,256]{1,0:T(8,128)(2,1)S(1)} %convolution_convert_fusion.1), channel_id=1, replica_groups=mesh['section'=2,'dp'=4,'tensor'=4] {'section','tensor'}, dimensions={1}, use_global_device_ids=true | all-gather | bytes 589824 | tf_op jit(solution)/shard_map/all_gather | solution.py:51
  72.9 9.0 %all_gather.20 = bf16[512,256]{1,0:T(8,128)(2,1)S(1)} all-gather(bf16[128,256]{1,0:T(8,128)(2,1)S(1)} %pad_maximum_fusion.1), channel_id=1, replica_groups=mesh['section'=2,'dp'=4,'tensor'=4] {'dp'}, dimensions={0}, use_global_device_ids=true | all-gather | bytes 327680 | tf_op jit(solution)/shard_map/all_gather | solution.py:56
  81.9 8.4 %convolution_bitcast_fusion = f32[16,8,8,128]{3,1,2,0:T(8,128)S(1)} fusion(bf16[8192,1024]{1,0:T(8,128)(2,1)} %param.11, bf16[128,8192]{1,0:T(8,128)(2,1)S(1)} %copy-done, f32[8192]{0:T(1024)S(1)} %convert_element_type.75, f32[128]{0:T(128)S(1)} %add_rsqrt_fusion.1), kind=kOutput, calls=%fused_computation.18 | convolution fusion | flops 2151677952 | bytes 19431936 | tf_op jit(solution)/shard_map/dot_general | solution.py:44
  94.3 4.9 fusion.33
  99.9 287.0 %all-gather.9.cloned.1.call-done = f32[1024,8192]{1,0:T(8,128)} async-done(((f32[128,8192]{1,0:T(8,128)}), f32[1024,8192]{1,0:T(8,128)}) %all-gather.9.cloned.1.call-update) | async-done | bytes 33554448 | tf_op jit(solution)/shard_map/all_gather | solution.py:77
  387.0 14.0 %reduce_sum.38 = f32[128,8192]{1,0:T(8,128)} reduce(f32[8,128,8192]{2,1,0:T(8,128)} %bitcast.53, f32[]{:T(128)} %constant.19.clone.1), dimensions={0}, to_apply=%region_3.4 | reduce | flops 7340032 | bytes 37748740 | tf_op jit(solution)/shard_map/reduce_sum | solution.py:77
  401.0 3.6 fusion
  404.6 1.9 fusion.2
  406.5 4.1 copy.32
  410.6 30.5 %all_to_all.38 = bf16[128,4,2048]{0,2,1:T(8,128)(2,1)} all-to-all(bf16[128,4,2048]{0,2,1:T(8,128)(2,1)} %bitcast.58), channel_id=1, replica_groups=mesh['section'=2,'dp'=4,'tensor'=4] {'dp'}, dimensions={1} | all-to-all | bytes 4194304 | tf_op jit(solution)/shard_map/all_to_all | solution.py:82
  441.1 4.0 copy.33
  445.1 8.5 %fusion.34 = f32[512,2048]{1,0:T(8,128)S(1)} fusion(bf16[512,2048]{1,0:T(8,128)(2,1)} %bitcast.62, bf16[2048,2048]{1,0:T(8,128)(2,1)} %param.15), kind=kOutput, calls=%fused_computation.64 | convolution fusion | flops 4294967296 | bytes 14680064 | tf_op jit(solution)/shard_map/dot_general | solution.py:86
  453.6 6.9 fusion.35
  460.5 3.8 pad_maximum_fusion
  464.3 83.1 %reduce-scatter.3.cloned.1.call-done = f32[128,4096]{1,0:T(8,128)} async-done(((f32[512,4096]{1,0:T(8,128)}), f32[128,4096]{1,0:T(8,128)}) %reduce-scatter.3.cloned.1.call-update) | async-done | bytes 2097168 | tf_op jit(solution)/shard_map/reduce_scatter | solution.py:88
  547.4 2.6 fusion.8
  550.2 35.3 %all-gather.7.cloned.1.call-done = bf16[512,2048]{1,0:T(8,128)(2,1)} async-done(((bf16[128,2048]{1,0:T(8,128)(2,1)}), bf16[512,2048]{1,0:T(8,128)(2,1)}) %all-gather.7.cloned.1.call-update) | async-done | bytes 2097168 | tf_op jit(solution)/shard_map/all_gather | solution.py:94
  585.4 10.5 %fusion.36 = f32[512,2048]{1,0:T(8,128)} fusion(bf16[512,2048]{1,0:T(8,128)(2,1)} %all-gather.7.cloned.1.call-done, bf16[2048,2048]{1,0:T(8,128)(2,1)} %param.17), kind=kOutput, calls=%fused_computation.66 | convolution fusion | flops 4294967296 | bytes 14680064 | tf_op jit(solution)/shard_map/dot_general | solution.py:98
  597.4 3.6 all-to-all-start
  601.0 24.9 %all-to-all-done = bf16[128,4,2048]{2,0,1:T(8,128)(2,1)S(1)} async-done(((bf16[128,4,2048]{2,0,1:T(8,128)(2,1)}), bf16[128,4,2048]{2,0,1:T(8,128)(2,1)S(1)}, u32[]{:S(2)}, u32[]{:S(2)}) %all-to-all-start) | async-done | bytes 2097184 | tf_op jit(solution)/shard_map/all_to_all | solution.py:81
  626.0 58.1 %reduce-scatter.5.cloned.1.call-done = f32[64,2048]{1,0:T(8,128)} async-done(((f32[512,2048]{1,0:T(8,128)}), f32[64,2048]{1,0:T(8,128)}) %reduce-scatter.5.cloned.1.call-update) | async-done | bytes 524304 | tf_op jit(solution)/shard_map/reduce_scatter | solution.py:97
  (47 shorter events, 9.9 us)
Async XLA Ops:
  6.5 34.3 %all-gather.5.cloned.1.call-start = ((), (), s32[]{:S(2)}) async-start(), calls=%async_computation.4 | async-start | bytes 2359296 | tf_op jit(solution)/shard_map/all_gather | solution.py:38
  7.3 379.7 %all-gather.9.cloned.1.call-start = ((), (), s32[]{:S(2)}) async-start(), calls=%async_computation.8 | async-start | bytes 37748736 | tf_op jit(solution)/shard_map/all_gather | solution.py:77
  42.9 39.0 %copy-start = (bf16[128,8192]{1,0:T(8,128)(2,1)S(1)}, bf16[128,8192]{1,0:T(8,128)(2,1)}, u32[]{:S(2)}) copy-start(bf16[128,8192]{1,0:T(8,128)(2,1)} %all-gather.5.cloned.1.call-done) | copy-start | bytes 6291460
  81.9 11.6 %slice-start = ((s8[16777216]{0:T(1024)(128)(4,1)}), s8[4194304]{0:T(1024)(128)(4,1)S(1)}, s32[]{:S(2)}) async-start(s8[16777216]{0:T(1024)(128)(4,1)} %bitcast.55), calls=%async_computation.9 | async-start | bytes 8388608
  81.9 11.6 %slice-start.1 = ((s8[16777216]{0:T(1024)(128)(4,1)}), s8[4194304]{0:T(1024)(128)(4,1)S(1)}, s32[]{:S(2)}) async-start(s8[16777216]{0:T(1024)(128)(4,1)} %bitcast.55), calls=%async_computation.10 | async-start | bytes 8388608
  81.9 11.6 %slice-start.2 = ((s8[16777216]{0:T(1024)(128)(4,1)}), s8[4194304]{0:T(1024)(128)(4,1)S(1)}, s32[]{:S(2)}) async-start(s8[16777216]{0:T(1024)(128)(4,1)} %bitcast.55), calls=%async_computation.11 | async-start | bytes 8388608
  92.1 2.2 slice-start.3
  99.2 0.7 copy-start.2
  99.2 448.2 %reduce-scatter.3.cloned.1.call-start = ((), (), s32[]{:S(2)}) async-start(), calls=%async_computation.5 | async-start | bytes 10485760 | tf_op jit(solution)/shard_map/reduce_scatter | solution.py:88
  445.1 8.5 %copy-start.1 = (bf16[4,128,2048]{2,1,0:T(8,128)(2,1)S(1)}, bf16[4,128,2048]{2,1,0:T(8,128)(2,1)}, u32[]{:S(2)}) copy-start(bf16[4,128,2048]{2,1,0:T(8,128)(2,1)} %copy.33) | copy-start | bytes 6291460
  464.3 121.2 %all-gather.7.cloned.1.call-start = ((), (), s32[]{:S(2)}) async-start(), calls=%async_computation.6 | async-start | bytes 2621440 | tf_op jit(solution)/shard_map/all_gather | solution.py:94
  550.1 133.9 %reduce-scatter.5.cloned.1.call-start = ((), (), s32[]{:S(2)}) async-start(), calls=%async_computation.7 | async-start | bytes 4718592 | tf_op jit(solution)/shard_map/reduce_scatter | solution.py:97
  597.4 28.6 %all-to-all-start = ((bf16[128,4,2048]{2,0,1:T(8,128)(2,1)}), bf16[128,4,2048]{2,0,1:T(8,128)(2,1)S(1)}, u32[]{:S(2)}, u32[]{:S(2)}) async-start(bf16[128,4,2048]{2,0,1:T(8,128)(2,1)} %bitcast.57), calls=%async_computation | async-start | bytes 4194304 | tf_op jit(solution)/shard_map/all_to_all | solution.py:81
Sparse Core Ops, SparseCore 0:
  8.9 31.8 all-gather.4
  99.4 287.5 all-gather.8
  464.4 83.0 reduce-scatter.2
  550.2 35.1 all-gather.6
  596.0 87.9 reduce-scatter.4
